TPU v7x, 32 devices: a whole 2x2x4 slice. The times are simulated.
32 devices in a mesh: dp: 16 (over z, x, core), tensor: 2 (over y).
Axes of the slice: x: 2, y: 2, z: 4, core: 2. Of those that a mesh axis runs over, the one named last changes fastest.
Arguments:
- query_rows: bfloat16 [6144, 5120], P('dp', 'tensor'), may hold values from -128 to 128
- key_rows: bfloat16 [6144, 5120], P('dp', 'tensor'), may hold values from -5 to 5
- value_rows: bfloat16 [6144, 5120], P('dp', 'tensor'), may hold values from -12 to 12
- action_mask: int32 [16, 384], P('dp'), may hold values from 0 to 1, as said below
- residual: bfloat16 [6144, 5120], P('dp', 'tensor'), may hold values from -100 to 100
- out_weight: bfloat16 [5120, 5120], P(None, 'tensor'), may hold values from -0.078125 to 0.078125
- norm_gain: float32 [5120], P('tensor'), may hold values from 0.1 to 1.9
- upstream: bfloat16 [6144, 5120], P('dp', 'tensor'), may hold values from -6 to 6
- residual_grad: bfloat16 [6144, 5120], P('dp', 'tensor'), may hold values from -2 to 2
Outputs:
- layer_out: bfloat16 [6144, 5120], P('dp', 'tensor')
- grad_residual: bfloat16 [6144, 5120], P('dp', 'tensor')
- grad_query: bfloat16 [6144, 5120], P('dp', 'tensor')
- grad_key: bfloat16 [6144, 5120], P('dp', 'tensor')
- grad_value: bfloat16 [6144, 5120], P('dp', 'tensor')
- grad_out_weight: float32 [5120, 5120], P('dp', 'tensor')
- grad_gain: float32 [5120], P('tensor')
Inputs may be any that keep to these rules, and one draw needn't show every extreme that they name: `action_mask`: each row is a run of zeros followed by a run of ones; the ones number 1 to 192.
All inputs are finite; a program needn't handle non-finite values.
Results may differ from a plain program's by a relative error of at most 0.015.
Values may be sent and summed in bfloat16 or wider, within the bound.
A program may use at most 192 MiB of HBM per device.

v0:
```python
import functools

import jax
import jax.numpy as jnp
from jax import lax
from jax.experimental import pallas as pl
from jax.experimental.pallas import tpu as pltpu
from jax.sharding import PartitionSpec as P

HEAD_DIM = 128
LEN = 384

epsilon = 1e-05
SCALE = HEAD_DIM ** (-0.5)
NT = (((1,), (1,)), ((), ()))
TN = (((0,), (0,)), ((), ()))


def dot(a, b, dims):
    return lax.dot_general(a, b, dims, preferred_element_type=jnp.float32)


def forward_kernel(heads, observed_ref, query_ref, key_ref, value_ref, probs_ref, attended_ref):
    observed = observed_ref[pl.program_id(0)]
    row = lax.broadcasted_iota(jnp.int32, (LEN, LEN), 0)
    column = lax.broadcasted_iota(jnp.int32, (LEN, LEN), 1)
    allowed = column <= jnp.maximum(row, observed - 1)
    for head in range(heads):
        span = slice(head * HEAD_DIM, (head + 1) * HEAD_DIM)
        scores = dot(query_ref[:, span], key_ref[:, span], NT) * SCALE
        masked = jnp.where(allowed, scores, -jnp.inf)
        weights = jnp.exp(masked - jnp.max(masked, axis=1, keepdims=True))
        probs = weights * (1.0 / jnp.sum(weights, axis=1, keepdims=True))
        low = probs.astype(jnp.bfloat16)
        probs_ref[head] = low
        attended_ref[:, span] = jnp.dot(
            low, value_ref[:, span], preferred_element_type=jnp.float32
        ).astype(jnp.bfloat16)


def backward_kernel(
    heads, probs_ref, query_ref, key_ref, value_ref, cotangent_ref, query_out, key_out, value_out
):
    for head in range(heads):
        span = slice(head * HEAD_DIM, (head + 1) * HEAD_DIM)
        low = probs_ref[head]
        cotangent = cotangent_ref[:, span]
        value_out[:, span] = dot(low, cotangent, TN).astype(jnp.bfloat16)
        grad_probs = dot(cotangent, value_ref[:, span], NT)
        probs = low.astype(jnp.float32)
        delta = jnp.sum(probs * grad_probs, axis=1, keepdims=True)
        grad_scores = (probs * (grad_probs - delta) * SCALE).astype(jnp.bfloat16)
        query_out[:, span] = jnp.dot(
            grad_scores, key_ref[:, span], preferred_element_type=jnp.float32
        ).astype(jnp.bfloat16)
        key_out[:, span] = dot(grad_scores, query_ref[:, span], TN).astype(jnp.bfloat16)


def head_group(head_count):
    return max(size for size in range(1, 6) if head_count % size == 0)


def specs(heads):
    rows = pl.BlockSpec((LEN, heads * HEAD_DIM), lambda s, h: (s, h))
    square = pl.BlockSpec((None, heads, LEN, LEN), lambda s, h: (s, h, 0, 0))
    return rows, square


def attend(observed, query_rows, key_rows, value_rows):
    tok_rows, width = query_rows.shape
    head_count, seq_count = width // HEAD_DIM, tok_rows // LEN
    heads = head_group(head_count)
    rows, square = specs(heads)
    pairs = seq_count * head_count * LEN * LEN
    return pl.pallas_call(
        functools.partial(forward_kernel, heads),
        grid=(seq_count, head_count // heads),
        in_specs=[pl.BlockSpec(memory_space=pltpu.SMEM), rows, rows, rows],
        out_specs=[square, rows],
        out_shape=[
            jax.ShapeDtypeStruct((seq_count, head_count, LEN, LEN), jnp.bfloat16),
            jax.ShapeDtypeStruct((tok_rows, width), jnp.bfloat16),
        ],
        cost_estimate=pl.CostEstimate(
            flops=4 * pairs * HEAD_DIM,
            bytes_accessed=2 * pairs + 8 * tok_rows * width,
            transcendentals=pairs,
        ),
        name="attend",
    )(observed, query_rows, key_rows, value_rows)


def attend_backward(probs, query_rows, key_rows, value_rows, cotangent):
    tok_rows, width = query_rows.shape
    head_count, seq_count = width // HEAD_DIM, tok_rows // LEN
    heads = head_group(head_count)
    rows, square = specs(heads)
    pairs = seq_count * head_count * LEN * LEN
    return pl.pallas_call(
        functools.partial(backward_kernel, heads),
        grid=(seq_count, head_count // heads),
        in_specs=[square, rows, rows, rows, rows],
        out_specs=[rows, rows, rows],
        out_shape=[jax.ShapeDtypeStruct((tok_rows, width), jnp.bfloat16)] * 3,
        cost_estimate=pl.CostEstimate(
            flops=8 * pairs * HEAD_DIM,
            bytes_accessed=2 * pairs + 14 * tok_rows * width,
            transcendentals=0,
        ),
        name="attend_backward",
    )(probs, query_rows, key_rows, value_rows, cotangent)


def sum_groups(groups, value):
    if groups & (groups - 1):
        return lax.psum(value, "dp")
    bit = 1
    while bit < groups:
        value = value + lax.ppermute(value, "dp", [(i, i ^ bit) for i in range(groups)])
        bit *= 2
    return value


def shards(
    groups,
    tensor_size,
    query_rows,
    key_rows,
    value_rows,
    action_mask,
    residual,
    out_weight,
    norm_gain,
    upstream,
    residual_grad,
):
    model_width = out_weight.shape[0]
    own_width = residual.shape[1]
    pair = tensor_size == 2
    swap = [(0, 1), (1, 0)]
    mine = lax.axis_index("tensor")

    def weight_rows(index):
        return lax.dynamic_slice_in_dim(out_weight, index * own_width, own_width, 0)

    def sum_pair(value):
        if pair:
            return value + lax.ppermute(value, "tensor", swap)
        return lax.psum(value, "tensor")

    observed = jnp.sum((action_mask == 0).astype(jnp.int32), axis=1)
    probs, attended = attend(observed, query_rows, key_rows, value_rows)
    attended_all = lax.all_gather(attended, "dp", axis=0, tiled=True)
    if pair:
        theirs = dot(attended, weight_rows(1 - mine), NT).astype(jnp.bfloat16)
        arriving = lax.ppermute(theirs, "tensor", swap)
        own = dot(attended, weight_rows(mine), NT)
        own_sum = own + arriving.astype(jnp.float32)
    else:
        own_sum = lax.psum_scatter(
            dot(attended, out_weight, NT), "tensor", scatter_dimension=1, tiled=True
        )
    layer_out = (own_sum + residual.astype(jnp.float32)).astype(jnp.bfloat16)
    out_float = layer_out.astype(jnp.float32)
    upstream_float = upstream.astype(jnp.float32)
    scaled = upstream_float * norm_gain[None, :]
    sums = sum_pair(
        jnp.stack([jnp.sum(out_float * out_float, axis=1), jnp.sum(scaled * out_float, axis=1)])
    )
    row_rms = jnp.sqrt(sums[0] / model_width + epsilon)[:, None]
    normed = out_float / row_rms
    row_inner = sums[1][:, None] / (row_rms * model_width)
    grad_residual = (
        residual_grad.astype(jnp.float32) + (scaled - normed * row_inner) / row_rms
    ).astype(jnp.bfloat16)
    if pair:
        other = lax.ppermute(grad_residual, "tensor", swap)
        first = mine == 0
        low_half = jnp.where(first, grad_residual, other)
        high_half = jnp.where(first, other, grad_residual)
        grad_full = jnp.concatenate([low_half, high_half], axis=1)
        grad_attended = jnp.dot(
            grad_residual, weight_rows(mine), preferred_element_type=jnp.float32
        ) + jnp.dot(other, weight_rows(1 - mine), preferred_element_type=jnp.float32)
    else:
        grad_full = lax.all_gather(grad_residual, "tensor", axis=1, tiled=True)
        grad_attended = jnp.dot(grad_full, out_weight, preferred_element_type=jnp.float32)
    grad_attended = grad_attended.astype(jnp.bfloat16)
    received = lax.all_to_all(grad_full, "dp", split_axis=1, concat_axis=0, tiled=True)
    gain_part = jnp.sum(upstream_float * normed, axis=0)
    grad_query, grad_key, grad_value = attend_backward(
        probs, query_rows, key_rows, value_rows, grad_attended
    )
    grad_query, gain_part = lax.optimization_barrier((grad_query, gain_part))
    grad_gain = sum_groups(groups, gain_part)
    grad_out_weight = dot(received, attended_all, TN)
    return layer_out, grad_residual, grad_query, grad_key, grad_value, grad_out_weight, grad_gain


def solution(mesh):
    rows = P("dp", "tensor")
    return jax.shard_map(
        functools.partial(shards, mesh.shape["dp"], mesh.shape["tensor"]),
        mesh=mesh,
        in_specs=(
            rows,
            rows,
            rows,
            P("dp", None),
            rows,
            P(None, "tensor"),
            P("tensor"),
            rows,
            rows,
        ),
        out_specs=(rows, rows, rows, rows, rows, rows, P("tensor")),
        check_vma=False,
    )
```

profile of v0, /device:TPU:27, one launch (start us, length us, event | category | flops | bytes accessed | tf_op | source)
XLA Modules:
  0.0 292.9 jit_solution(4896069805837783981)
XLA Ops:
  7.2 1.3 fusion.24
  8.5 13.0 %attend.1 = (bf16[1,20,384,384]{3,2,1,0:T(8,128)(2,1)}, bf16[384,2560]{1,0:T(8,128)(2,1)}) custom-call(s32[1]{0:T(128)} %bitcast.observed_ref, bf16[384,2560]{1,0:T(8,128)(2,1)} %query_ref.3, bf16[384,2560]{1,0:T(8,128)(2,1)} %key_ref.3, bf16[384,2560]{1,0:T(8,128)(2,1)} %value_ref.3), custom_call_target="tpu_custom_call" | custom-call | flops 1509949440 | bytes 13762560 | tf_op jit(solution)/shard_map/attend/pallas_call | solution.py:75
  21.6 14.9 %fusion.15 = bf16[384,2560]{1,0:T(8,128)(2,1)} fusion(bf16[384,2560]{1,0:T(8,128)(2,1)} %get-tuple-element.14, bf16[5120,2560]{1,0:T(8,128)(2,1)} %param.14, s32[]{:T(128)S(6)} %select_n.21), kind=kOutput, calls=%fused_computation.16 | convolution fusion | flops 5034147840 | bytes 17039364 | tf_op jit(solution)/shard_map/dot_general | solution.py:20
  36.5 1.2 collective-permute-start
  37.7 42.8 %collective-permute-done = bf16[384,2560]{1,0:T(8,128)(2,1)} collective-permute-done((bf16[384,2560]{1,0:T(8,128)(2,1)}, bf16[384,2560]{1,0:T(8,128)(2,1)}, u32[]{:S(2)}, u32[]{:S(2)}) %collective-permute-start) | collective-permute-done | bytes 1966112 | tf_op jit(solution)/shard_map/ppermute | solution.py:156
  80.5 19.3 %fusion.21 = (f32[384]{0:T(512)S(1)}, f32[384]{0:T(512)S(1)}, bf16[384,2560]{1,0:T(8,128)(2,1)S(1)}) fusion(f32[2560]{0:T(1024)S(1)} %copy-done.5, bf16[384,2560]{1,0:T(8,128)(2,1)} %param.16, bf16[384,2560]{1,0:T(8,128)(2,1)} %param.13, bf16[384,2560]{1,0:T(8,128)(2,1)} %collective-permute-done, bf16[384,2560]{1,0:T(8,128)(2,1)S(1)} %copy-done.1, ...), kind=kOutput, calls=%fused_computation.20 | convolution fusion | flops 5044960256 | bytes 22950916 | tf_op jit(solution)/shard_map/dot_general | solution.py:20
  99.9 1.3 collective-permute-start.1
  101.2 1.6 collective-permute-done.1
  102.8 2.0 fusion.20
  104.9 1.3 collective-permute-start.2
  106.2 40.9 %collective-permute-done.2 = bf16[384,2560]{1,0:T(8,128)(2,1)} collective-permute-done((bf16[384,2560]{1,0:T(8,128)(2,1)S(1)}, bf16[384,2560]{1,0:T(8,128)(2,1)}, u32[]{:S(2)}, u32[]{:S(2)}) %collective-permute-start.2) | collective-permute-done | bytes 1966112 | tf_op jit(solution)/shard_map/ppermute | solution.py:177
  147.1 1.8 broadcast_select_fusion.1
  149.0 2.3 pad_maximum_fusion
  151.3 6.3 %copy.16 = bf16[384,5120]{0,1:T(8,128)(2,1)} copy(bf16[384,5120]{1,0:T(8,128)(2,1)} %pad_maximum_fusion) | data formatting | bytes 7864320 | tf_op jit(solution)/shard_map/concatenate | solution.py:181
  157.6 8.8 %all-to-all-start = ((bf16[384,16,320]{0,2,1:T(8,128)(2,1)}), bf16[384,16,320]{0,2,1:T(8,128)(2,1)}, u32[]{:S(2)}, u32[]{:S(2)}) async-start(bf16[384,16,320]{0,2,1:T(8,128)(2,1)} %bitcast.11), calls=%async_computation | async-start | bytes 7864320 | tf_op jit(solution)/shard_map/all_to_all | solution.py:189
  166.4 8.5 %fusion.4 = f32[384,2560]{1,0:T(8,128)S(1)} fusion(bf16[384,2560]{1,0:T(8,128)(2,1)S(1)} %get-tuple-element.26, bf16[5120,2560]{1,0:T(8,128)(2,1)} %param.14, s32[]{:T(128)S(6)} %select_n.20), kind=kOutput, calls=%fused_computation.4 | convolution fusion | flops 5033164800 | bytes 19005444 | tf_op jit(solution)/shard_map/dot_general | solution.py:182
  174.9 11.6 %fusion.12.cotangent_ref = bf16[384,2560]{1,0:T(8,128)(2,1)} fusion(f32[384,2560]{1,0:T(8,128)S(1)} %fusion.4, bf16[384,2560]{1,0:T(8,128)(2,1)} %collective-permute-done.2, bf16[5120,2560]{1,0:T(8,128)(2,1)} %param.14, s32[]{:T(128)S(6)} %select_n.21), kind=kOutput, calls=%fused_computation.15 | convolution fusion | flops 5035130880 | bytes 20971524 | tf_op jit(solution)/shard_map/dot_general | solution.py:184
  186.5 13.9 %attend_backward.1 = (bf16[384,2560]{1,0:T(8,128)(2,1)}, bf16[384,2560]{1,0:T(8,128)(2,1)}, bf16[384,2560]{1,0:T(8,128)(2,1)}) custom-call(bf16[1,20,384,384]{3,2,1,0:T(8,128)(2,1)} %get-tuple-element.15.probs_ref, bf16[384,2560]{1,0:T(8,128)(2,1)} %query_ref.3, bf16[384,2560]{1,0:T(8,128)(2,1)} %key_ref.3, bf16[384,2560]{1,0:T(8,128)(2,1)} %value_ref.3, ...), custom_call_target="tpu_custom_call" | custom-call | flops 3019898880 | bytes 19660800 | tf_op jit(solution)/shard_map/attend_backward/pallas_call | solution.py:99
  201.7 8.1 %collective-permute-done.4 = f32[2560]{0:T(1024)S(1)} collective-permute-done((f32[2560]{0:T(1024)S(1)}, f32[2560]{0:T(1024)S(1)}, u32[]{:S(2)}, u32[]{:S(2)}) %collective-permute-start.4) | collective-permute-done | bytes 10272 | tf_op jit(solution)/shard_map/ppermute | solution.py:119
  209.9 30.5 %collective-permute-done.5 = f32[2560]{0:T(1024)S(1)} collective-permute-done((f32[2560]{0:T(1024)S(1)}, f32[2560]{0:T(1024)S(1)}, u32[]{:S(2)}, u32[]{:S(2)}) %collective-permute-start.5) | collective-permute-done | bytes 10272 | tf_op jit(solution)/shard_map/ppermute | solution.py:119
  240.4 2.2 collective-permute-start.6
  242.6 19.9 %collective-permute-done.6 = f32[2560]{0:T(1024)S(1)} collective-permute-done((f32[2560]{0:T(1024)S(1)}, f32[2560]{0:T(1024)S(1)}, u32[]{:S(2)}, u32[]{:S(2)}) %collective-permute-start.6) | collective-permute-done | bytes 10272 | tf_op jit(solution)/shard_map/ppermute | solution.py:119
  263.1 4.7 %copy.18 = bf16[16,40,8,384]{3,2,0,1:T(8,128)(2,1)} copy(bf16[16,40,8,384]{3,2,1,0:T(8,128)(2,1)} %bitcast.3) | data formatting | bytes 7864320 | tf_op jit(solution)/shard_map/all_to_all | solution.py:189
  267.8 18.2 %fusion.35 = f32[320,2560]{1,0:T(8,128)} fusion(bf16[6144,320]{0,1:T(8,128)(2,1)} %bitcast.12, bf16[6144,2560]{1,0:T(8,128)(2,1)} %all-gather.2.cloned.1.call-done), kind=kOutput, calls=%fused_computation.41 | convolution fusion | flops 10066329600 | bytes 38666240 | tf_op jit(solution)/shard_map/dot_general | solution.py:20
  (30 shorter events, 2.1 us)
Async XLA Ops:
  7.2 260.6 %all-gather.2.cloned.1.call-start = ((), (), s32[]{:S(2)}) async-start(), calls=%async_computation.1 | async-start | bytes 33423360 | tf_op jit(solution)/shard_map/all_gather | solution.py:153
  21.6 58.9 %copy-start.1 = (bf16[384,2560]{1,0:T(8,128)(2,1)S(1)}, bf16[384,2560]{1,0:T(8,128)(2,1)}, u32[]{:S(2)}) copy-start(bf16[384,2560]{1,0:T(8,128)(2,1)} %get-tuple-element.14) | copy-start | bytes 5898244
  21.6 58.9 %copy-start.5 = (f32[2560]{0:T(1024)S(1)}, f32[2560]{0:T(1024)}, u32[]{:S(2)}) copy-start(f32[2560]{0:T(1024)} %param.15) | copy-start | bytes 30724
  36.5 44.0 %collective-permute-start = (bf16[384,2560]{1,0:T(8,128)(2,1)}, bf16[384,2560]{1,0:T(8,128)(2,1)}, u32[]{:S(2)}, u32[]{:S(2)}) collective-permute-start(bf16[384,2560]{1,0:T(8,128)(2,1)} %fusion.15), channel_id=1, source_target_pairs={{0,1},{1,0},{2,3},{3,2},{4,5},{5,4},{6,7},{7,6},{8,9},{9,8},{10,11... | collective-permute-start | bytes 5898248 | tf_op jit(solution)/shard_map/ppermute | solution.py:156
  37.7 65.1 %copy-start.2 = (bf16[384,2560]{1,0:T(8,128)(2,1)S(1)}, bf16[384,2560]{1,0:T(8,128)(2,1)}, u32[]{:S(2)}) copy-start(bf16[384,2560]{1,0:T(8,128)(2,1)} %param.16) | copy-start | bytes 5898244
  37.7 65.1 %copy-start.3 = (bf16[384,2560]{1,0:T(8,128)(2,1)S(1)}, bf16[384,2560]{1,0:T(8,128)(2,1)}, u32[]{:S(2)}) copy-start(bf16[384,2560]{1,0:T(8,128)(2,1)} %param.17) | copy-start | bytes 5898244
  99.8 5.0 %copy-start.4 = (bf16[384,2560]{1,0:T(8,128)(2,1)}, bf16[384,2560]{1,0:T(8,128)(2,1)S(1)}, u32[]{:S(2)}) copy-start(bf16[384,2560]{1,0:T(8,128)(2,1)S(1)} %get-tuple-element.29) | copy-start | bytes 5898244
  99.9 2.9 collective-permute-start.1
  104.9 61.5 %copy-start = (bf16[384,2560]{1,0:T(8,128)(2,1)}, bf16[384,2560]{1,0:T(8,128)(2,1)S(1)}, u32[]{:S(2)}) copy-start(bf16[384,2560]{1,0:T(8,128)(2,1)S(1)} %get-tuple-element.26) | copy-start | bytes 5898244
  104.9 42.2 %collective-permute-start.2 = (bf16[384,2560]{1,0:T(8,128)(2,1)S(1)}, bf16[384,2560]{1,0:T(8,128)(2,1)}, u32[]{:S(2)}, u32[]{:S(2)}) collective-permute-start(bf16[384,2560]{1,0:T(8,128)(2,1)S(1)} %get-tuple-element.26), channel_id=1, source_target_pairs={{0,1},{1,0},{2,3},{3,2},{4,5},{5,4},{6,7},{7,6},{8,9},{9,8},{10,11... | collective-permute-start | bytes 5898248 | tf_op jit(solution)/shard_map/ppermute | solution.py:177
  157.6 105.6 %all-to-all-start = ((bf16[384,16,320]{0,2,1:T(8,128)(2,1)}), bf16[384,16,320]{0,2,1:T(8,128)(2,1)}, u32[]{:S(2)}, u32[]{:S(2)}) async-start(bf16[384,16,320]{0,2,1:T(8,128)(2,1)} %bitcast.11), calls=%async_computation | async-start | bytes 7864320 | tf_op jit(solution)/shard_map/all_to_all | solution.py:189
  200.4 1.2 collective-permute-start.3
  201.6 8.3 %collective-permute-start.4 = (f32[2560]{0:T(1024)S(1)}, f32[2560]{0:T(1024)S(1)}, u32[]{:S(2)}, u32[]{:S(2)}) collective-permute-start(f32[2560]{0:T(1024)S(1)} %add.58), channel_id=1, source_target_pairs={{0,4},{2,6},{4,0},{6,2},{8,12},{10,14},{12,8},{14,10},{16,20},{18,... | collective-permute-start | bytes 30728 | tf_op jit(solution)/shard_map/ppermute | solution.py:119
  209.8 30.5 %collective-permute-start.5 = (f32[2560]{0:T(1024)S(1)}, f32[2560]{0:T(1024)S(1)}, u32[]{:S(2)}, u32[]{:S(2)}) collective-permute-start(f32[2560]{0:T(1024)S(1)} %add.59), channel_id=1, source_target_pairs={{0,8},{2,10},{4,12},{6,14},{8,0},{10,2},{12,4},{14,6},{16,24},{18,... | collective-permute-start | bytes 30728 | tf_op jit(solution)/shard_map/ppermute | solution.py:119
  240.4 22.1 %collective-permute-start.6 = (f32[2560]{0:T(1024)S(1)}, f32[2560]{0:T(1024)S(1)}, u32[]{:S(2)}, u32[]{:S(2)}) collective-permute-start(f32[2560]{0:T(1024)S(1)} %add.60), channel_id=1, source_target_pairs={{0,16},{2,18},{4,20},{6,22},{8,24},{10,26},{12,28},{14,30},{16,0},... | collective-permute-start | bytes 30728 | tf_op jit(solution)/shard_map/ppermute | solution.py:119
Sparse Core Ops, SparseCore 0:
  21.7 173.4 all-gather.1
where the time goes:
time: 297 us; the launch traced here: 293 us
  waiting for transfers between devices  145 us (49%)
  matrix products  72.5 us (24%)
  Pallas kernels  26.9 us (9%)
  starting transfers between devices  15.3 us (5%)
  between operations  14.2 us (5%)
  local copies, waits for them, and re-layouts  11 us (4%)
  other arithmetic  8.16 us (3%)
    ppermute x4, waiting for transfers between devices, sum_groups(): lax.ppermute(value, 'dp', [(i, i ^ bit) for i in range(groups)])  59.5 us
    dot_general x3, matrix products, dot(): return lax.dot_general(a, b, dims, preferred_element_type=jnp.float32)  52.4 us
    ppermute x1, waiting for transfers between devices, shards(): arriving = lax.ppermute(theirs, 'tensor', swap)  42.8 us
    ppermute x1, waiting for transfers between devices, shards(): other = lax.ppermute(grad_residual, 'tensor', swap)  40.9 us
    pallas_call x1, Pallas kernels, attend_backward(): pl.pallas_call(functools.partial(backward_kernel, heads), grid=(seq_count...  13.9 us
    pallas_call x1, Pallas kernels, attend(): pl.pallas_call(functools.partial(forward_kernel, heads), grid=(seq_count,...  13 us
    dot_general x1, matrix products, shards(): jnp.dot(other, weight_rows(1 - mine), preferred_element_type=jnp.float32)  11.6 us
    all_to_all x1, starting transfers between devices, shards(): lax.all_to_all(grad_full, 'dp', split_axis=1, concat_axis=0, tiled=True)  8.79 us
  transfers between devices with their start and end apart: 9, of which 7 were waited for; matrix products, arithmetic and copies ran while one was open for 25% of the time, Pallas kernels for 5%

commit v1 on v0

--- a/solution.py
+++ b/solution.py
@@ -111,6 +111,494 @@
     )(probs, query_rows, key_rows, value_rows, cotangent)
 
 
+MESH = pl.DeviceIdType.MESH
+
+
+def trunk_kernel(
+    groups,
+    att_h,
+    res_h,
+    ups_h,
+    rg_h,
+    gain_ref,
+    w_h,
+    probs_h,
+    q_h,
+    k_h,
+    v_h,
+    lo_h,
+    gr_h,
+    gq_h,
+    gk_h,
+    gv_h,
+    gw_h,
+    gain_o,
+    gath,
+    att_v,
+    ups_v,
+    rg_v,
+    theirs,
+    arrived,
+    lo_v,
+    gr_v,
+    turned,
+    turned_other,
+    other_v,
+    pieces,
+    sums_mine,
+    sums_theirs,
+    gain_v,
+    mid_out,
+    mid_in,
+    load_sem,
+    w_sem,
+    p_sems,
+    g_sems,
+    s_sems,
+    ag_sems,
+    piece_sems,
+    gain_sems,
+    mid_sems,
+    block_sem,
+    fetch_sem,
+    out_sem,
+    final_sem,
+):
+    rows, width = att_v.shape
+    model = 2 * width
+    chips = 4
+    part = width // chips
+    own_rows = part // 2
+    half = width // 2
+    d = lax.axis_index("dp")
+    t = lax.axis_index("tensor")
+    c = d % 2
+    x = (d // 2) % 2
+    zp = (d // 4) % 2
+    zh = d // 8
+
+    def device(zh_, zp_, x_, c_, t_):
+        return (((zh_ * 2 + zp_) * 2 + x_) * 2 + c_, t_)
+
+    y_peer = (d, 1 - t)
+    x_peer = device(zh, zp, 1 - x, c, t)
+    z_peer = device(zh, 1 - zp, x, c, t)
+    core_peer = device(zh, zp, x, 1 - c, t)
+    mid_peer = device(1 - zh, zp, x, c, t)
+
+    def remote(src, dst, sems, index, target):
+        return pltpu.make_async_remote_copy(
+            src_ref=src,
+            dst_ref=dst,
+            send_sem=sems.at[(0,) + index],
+            recv_sem=sems.at[(1,) + index],
+            device_id=target,
+            device_id_type=MESH,
+        )
+
+    barrier = pltpu.get_barrier_semaphore()
+    for r in range(1, groups):
+        pl.semaphore_signal(barrier, inc=1, device_id=((d + r) % groups, t), device_id_type=MESH)
+    pl.semaphore_signal(barrier, inc=1, device_id=y_peer, device_id_type=MESH)
+
+    def gather(src, slot, side, target):
+        cols = slice(side * half, (side + 1) * half)
+        return remote(src.at[:, cols], gath.at[slot, :, cols], ag_sems, (slot, side), target)
+
+    def piece(kind, source, k, dc):
+        kz, kx = k // 2, k % 2
+        dz = zp + kz - 2 * zp * kz
+        dx = x + kx - 2 * x * kx
+        core = c + dc - 2 * c * dc
+        delta = dz * 4 + dx * 2 + dc
+        src = source.at[k, pl.ds(core * own_rows, own_rows), :]
+        dst = pieces.at[kind, :, pl.ds(pl.multiple_of(delta * rows, 128), rows)]
+        far = remote(src, dst, piece_sems, (kind, delta), device(zh, kz, kx, core, t))
+        if dc == 1:
+            far.start()
+        else:
+
+            @pl.when(dz + dx > 0)
+            def _():
+                far.start()
+
+            @pl.when(dz + dx == 0)
+            def _():
+                pltpu.make_async_copy(src, pieces.at[kind, :, 0:rows], piece_sems.at[1, kind, 0]).start()
+
+    def projection(wp, res_v):
+        def w_load(side, k):
+            start = pl.multiple_of(side * width + k * part, part)
+            return pltpu.make_async_copy(w_h.at[pl.ds(start, part), :], wp.at[k], w_sem.at[k])
+
+        att_load = pltpu.make_async_copy(att_h, att_v, load_sem.at[0])
+        att_load.start()
+        for k in range(chips):
+            w_load(1 - t, k).start()
+        later = [
+            pltpu.make_async_copy(a, b, load_sem.at[i + 1])
+            for i, (a, b) in enumerate(((res_h, res_v), (ups_h, ups_v), (rg_h, rg_v)))
+        ]
+        for copy in later:
+            copy.start()
+        pl.semaphore_wait(barrier, groups)
+        gather(att_h, 4, 0, z_peer).start()
+        gather(att_h, 2, 1, x_peer).start()
+        gather(att_h, 4, 1, z_peer).start()
+        gather(att_h, 2, 0, x_peer).start()
+        for side in (0, 1):
+            gather(att_h, 1, side, core_peer).start()
+        att_load.wait()
+
+        def give(k, carry):
+            w_load(1 - t, k).wait()
+            theirs[k] = dot(att_v[...], wp[k], NT).astype(jnp.bfloat16)
+            remote(theirs.at[k], arrived.at[k], p_sems, (k,), y_peer).start()
+            w_load(t, k).start()
+            return carry
+
+        lax.fori_loop(0, chips, give, 0)
+        for copy in later:
+            copy.wait()
+
+        def take(k, carry):
+            squares, inner = carry
+            cols = pl.ds(pl.multiple_of(k * part, 128), part)
+            w_load(t, k).wait()
+            own = dot(att_v[...], wp[k], NT)
+            remote(theirs.at[k], arrived.at[k], p_sems, (k,), y_peer).wait()
+            total = own + arrived[k].astype(jnp.float32)
+            low = (total + res_v[:, cols].astype(jnp.float32)).astype(jnp.bfloat16)
+            lo_v[:, cols] = low
+            out = low.astype(jnp.float32)
+            scaled = ups_v[:, cols].astype(jnp.float32) * gain_ref[:, cols]
+            squares = squares + jnp.sum(out * out, axis=1, keepdims=True)
+            inner = inner + jnp.sum(scaled * out, axis=1, keepdims=True)
+            return squares, inner
+
+        zero = jnp.zeros((rows, 1), jnp.float32)
+        carry = lax.fori_loop(0, 2, take, (zero, zero))
+        gather(att_h, 4, 0, z_peer).wait_recv()
+        gather(gath.at[4], 6, 0, x_peer).start()
+        gather(att_h, 2, 1, x_peer).wait_recv()
+        gather(gath.at[2], 6, 1, z_peer).start()
+        squares, inner = lax.fori_loop(2, chips, take, carry)
+        lane = lax.broadcasted_iota(jnp.int32, (rows, 128), 1)
+        packed = jnp.where(lane == 0, squares, jnp.where(lane == 1, inner, 0.0))
+        sums_mine[...] = jnp.transpose(packed)[0:8]
+
+    pl.run_scoped(
+        projection,
+        pltpu.VMEM((chips, part, width), jnp.bfloat16),
+        pltpu.VMEM((rows, width), jnp.bfloat16),
+    )
+    exchange = remote(sums_mine, sums_theirs, s_sems, (0,), y_peer)
+    exchange.start()
+    lo_out = pltpu.make_async_copy(lo_v, lo_h, load_sem.at[0])
+    lo_out.start()
+    exchange.wait()
+    both = sums_mine[...] + sums_theirs[...]
+    wide = jnp.transpose(jnp.concatenate([both, jnp.zeros((120, rows), jnp.float32)], axis=0))
+    squares, inner = wide[:, 0:1], wide[:, 1:2]
+    rms = jnp.sqrt(squares / model + epsilon)
+    inverse = 1.0 / rms
+    row_inner = inner / (rms * model)
+    slope = row_inner * inverse
+
+    def normalise(k, carry):
+        cols = pl.ds(pl.multiple_of(k * part, 128), part)
+        out = lo_v[:, cols].astype(jnp.float32)
+        ups = ups_v[:, cols].astype(jnp.float32)
+        scaled = ups * gain_ref[:, cols]
+        grad = (rg_v[:, cols].astype(jnp.float32) + (scaled - out * slope) * inverse).astype(jnp.bfloat16)
+        gr_v[:, cols] = grad
+        turned[k] = jnp.transpose(grad.astype(jnp.float32)).astype(jnp.bfloat16)
+        gain_v[d, :, cols] = jnp.sum(ups * (out * inverse), axis=0, keepdims=True)
+        remote(turned.at[k], turned_other.at[k], g_sems, (k,), y_peer).start()
+        for dc in (0, 1):
+            piece(0, turned, k, dc)
+        return carry
+
+    lax.fori_loop(0, chips, normalise, 0)
+    gr_out = pltpu.make_async_copy(gr_v, gr_h, load_sem.at[1])
+    gr_out.start()
+
+    def gain_copy(r, sender):
+        return remote(gain_v.at[sender], gain_v.at[sender], gain_sems, (r,), ((d + r) % groups, t))
+
+    for r in range(1, groups):
+        gain_copy(r, d).start()
+    for side in (0, 1):
+        if side == 1:
+            gather(att_h, 4, 1, z_peer).wait_recv()
+        gather(gath.at[4], 5, side, core_peer).start()
+        if side == 0:
+            gather(att_h, 2, 0, x_peer).wait_recv()
+        gather(gath.at[2], 3, side, core_peer).start()
+
+    def pass_on(k, carry):
+        remote(turned.at[k], turned_other.at[k], g_sems, (k,), y_peer).wait()
+        for dc in (0, 1):
+            piece(1, turned_other, k, dc)
+        cols = pl.ds(pl.multiple_of(k * part, 128), part)
+        other_v[:, cols] = jnp.transpose(turned_other[k].astype(jnp.float32)).astype(jnp.bfloat16)
+        return carry
+
+    lax.fori_loop(0, 2, pass_on, 0)
+    for side in (0, 1):
+        gather(gath.at[4], 6, side, x_peer).wait_recv()
+        gather(gath.at[6], 7, side, core_peer).start()
+    lax.fori_loop(2, chips, pass_on, 0)
+    for slot in (1, 3, 5, 7):
+        for side in (0, 1):
+            gather(att_h, slot, side, core_peer).wait_recv()
+
+    blocks = width // part
+    keeps_first = (zh + t) % 2 == 0
+
+    def finish(kept, att_b):
+        def block_load(cb, slot):
+            cols = pl.ds(pl.multiple_of(cb * part, 128), part)
+            copies = [
+                pltpu.make_async_copy(
+                    att_h.at[:, cols], att_b.at[slot, 0:rows, :], block_sem.at[slot, 0]
+                )
+            ]
+            for delta in range(1, 8):
+                copies.append(
+                    pltpu.make_async_copy(
+                        gath.at[delta, :, cols],
+                        att_b.at[slot, delta * rows : (delta + 1) * rows, :],
+                        block_sem.at[slot, delta],
+                    )
+                )
+            return copies
+
+        def mid_copy(cb):
+            return remote(mid_out.at[cb], mid_in.at[cb], mid_sems, (cb,), mid_peer)
+
+        for copy in block_load(0, 0):
+            copy.start()
+        for kind in (0, 1):
+            for delta in range(8):
+                pltpu.make_async_copy(
+                    turned.at[0, 0:own_rows, :],
+                    pieces.at[kind, :, delta * rows : (delta + 1) * rows],
+                    piece_sems.at[1, kind, delta],
+                ).wait()
+            keeps = keeps_first if kind == 0 else jnp.logical_not(keeps_first)
+
+            def product(cb, carry, kind=kind, keeps=keeps):
+                slot = cb % 2
+                if kind == 0:
+                    for copy in block_load((cb + 1) % blocks, 1 - slot):
+                        copy.start()
+                else:
+
+                    @pl.when(cb + 1 < blocks)
+                    def _():
+                        for copy in block_load(cb + 1, 1 - slot):
+                            copy.start()
+
+                for copy in block_load(cb, slot):
+                    copy.wait()
+                value = jnp.dot(pieces[kind], att_b[slot], preferred_element_type=jnp.float32)
+
+                @pl.when(keeps)
+                def _():
+                    kept[cb] = value
+
+                @pl.when(jnp.logical_not(keeps))
+                def _():
+                    mid_out[cb] = value.astype(jnp.bfloat16)
+                    mid_copy(cb).start()
+
+                return carry
+
+            lax.fori_loop(0, blocks, product, 0)
+
+        def attention(pb, qb, kb, vb, wc, ob):
+            steps = width // (2 * HEAD_DIM)
+
+            def fetch(i, slot):
+                cols = pl.ds(pl.multiple_of(i * 2 * HEAD_DIM, 128), 2 * HEAD_DIM)
+                pairs = (
+                    (probs_h.at[pl.ds(2 * i, 2)], pb),
+                    (q_h.at[:, cols], qb),
+                    (k_h.at[:, cols], kb),
+                    (v_h.at[:, cols], vb),
+                    (w_h.at[:, cols], wc),
+                )
+                return [
+                    pltpu.make_async_copy(a, b.at[slot], fetch_sem.at[slot, j])
+                    for j, (a, b) in enumerate(pairs)
+                ]
+
+            def emit(i, slot):
+                cols = pl.ds(pl.multiple_of(i * 2 * HEAD_DIM, 128), 2 * HEAD_DIM)
+                return [
+                    pltpu.make_async_copy(ob.at[slot, j], b.at[:, cols], out_sem.at[slot, j])
+                    for j, b in enumerate((gq_h, gk_h, gv_h))
+                ]
+
+            for copy in fetch(0, 0):
+                copy.start()
+
+            def step(i, carry):
+                slot = i % 2
+
+                @pl.when(i + 1 < steps)
+                def _():
+                    for copy in fetch(i + 1, 1 - slot):
+                        copy.start()
+
+                for copy in fetch(i, slot):
+                    copy.wait()
+
+                @pl.when(i >= 2)
+                def _():
+                    for copy in emit(i - 2, slot):
+                        copy.wait()
+
+                mine = wc[slot, pl.ds(pl.multiple_of(t * width, 128), width), :]
+                other = wc[slot, pl.ds(pl.multiple_of((1 - t) * width, 128), width), :]
+                cotangents = (
+                    jnp.dot(gr_v[...], mine, preferred_element_type=jnp.float32)
+                    + jnp.dot(other_v[...], other, preferred_element_type=jnp.float32)
+                ).astype(jnp.bfloat16)
+                for j in range(2):
+                    span = slice(j * HEAD_DIM, (j + 1) * HEAD_DIM)
+                    low = pb[slot, j]
+                    cotangent = cotangents[:, span]
+                    ob[slot, 2, :, span] = dot(low, cotangent, TN).astype(jnp.bfloat16)
+                    grad_probs = dot(cotangent, vb[slot, :, span], NT)
+                    probs = low.astype(jnp.float32)
+                    delta = jnp.sum(probs * grad_probs, axis=1, keepdims=True)
+                    grad_scores = (probs * (grad_probs - delta) * SCALE).astype(jnp.bfloat16)
+                    ob[slot, 0, :, span] = jnp.dot(
+                        grad_scores, kb[slot, :, span], preferred_element_type=jnp.float32
+                    ).astype(jnp.bfloat16)
+                    ob[slot, 1, :, span] = dot(grad_scores, qb[slot, :, span], TN).astype(
+                        jnp.bfloat16
+                    )
+                for copy in emit(i, slot):
+                    copy.start()
+                return carry
+
+            lax.fori_loop(0, steps, step, 0)
+            for i in (steps - 2, steps - 1):
+                for copy in emit(i, i % 2):
+                    copy.wait()
+
+        two = 2 * HEAD_DIM
+        pl.run_scoped(
+            attention,
+            pltpu.VMEM((2, 2, rows, rows), jnp.bfloat16),
+            pltpu.VMEM((2, rows, two), jnp.bfloat16),
+            pltpu.VMEM((2, rows, two), jnp.bfloat16),
+            pltpu.VMEM((2, rows, two), jnp.bfloat16),
+            pltpu.VMEM((2, model, two), jnp.bfloat16),
+            pltpu.VMEM((2, 3, rows, two), jnp.bfloat16),
+        )
+        for r in range(1, groups):
+            gain_copy(r, (d + groups - r) % groups).wait()
+        total = gain_v[0]
+        for i in range(1, groups):
+            total = total + gain_v[i]
+        gain_o[...] = total
+
+        def close(cb, carry):
+            mid_copy(cb).wait()
+            kept[cb] = kept[cb] + mid_in[cb].astype(jnp.float32)
+            cols = pl.ds(pl.multiple_of(cb * part, 128), part)
+            pltpu.make_async_copy(kept.at[cb], gw_h.at[:, cols], final_sem.at[cb]).start()
+            return carry
+
+        lax.fori_loop(0, blocks, close, 0)
+        for cb in range(blocks):
+            cols = slice(cb * part, (cb + 1) * part)
+            pltpu.make_async_copy(kept.at[cb], gw_h.at[:, cols], final_sem.at[cb]).wait()
+
+    pl.run_scoped(
+        finish,
+        pltpu.VMEM((blocks, own_rows, part), jnp.float32),
+        pltpu.VMEM((2, 8 * rows, part), jnp.bfloat16),
+    )
+    lo_out.wait()
+    gr_out.wait()
+    for slot in range(1, 8):
+        for side in (0, 1):
+            gather(att_h, slot, side, core_peer).wait_send()
+    for kind in (0, 1):
+        for delta in range(1, 8):
+            remote(
+                turned.at[0, 0:own_rows, :],
+                pieces.at[kind, :, 0:rows],
+                piece_sems,
+                (kind, delta),
+                core_peer,
+            ).wait_send()
+
+
+def trunk(groups, att, res, ups, rg, gain, weight, probs, q, k, v):
+    rows, width = att.shape
+    model = weight.shape[0]
+    chips = 4
+    part = width // chips
+    own_rows = part // 2
+    anywhere = pl.BlockSpec(memory_space=pl.ANY)
+    local = pl.BlockSpec(memory_space=pltpu.VMEM)
+    low = jnp.bfloat16
+    act = jax.ShapeDtypeStruct((rows, width), low)
+    dma = pltpu.SemaphoreType.DMA
+    return pl.pallas_call(
+        functools.partial(trunk_kernel, groups),
+        in_specs=[anywhere] * 4 + [local] + [anywhere] * 5,
+        out_specs=[anywhere] * 6 + [local, anywhere],
+        out_shape=[act] * 5
+        + [
+            jax.ShapeDtypeStruct((own_rows, width), jnp.float32),
+            jax.ShapeDtypeStruct((1, width), jnp.float32),
+            jax.ShapeDtypeStruct((8, rows, width), low),
+        ],
+        scratch_shapes=[
+            pltpu.VMEM((rows, width), low),
+            pltpu.VMEM((rows, width), low),
+            pltpu.VMEM((rows, width), low),
+            pltpu.VMEM((chips, rows, part), low),
+            pltpu.VMEM((chips, rows, part), low),
+            pltpu.VMEM((rows, width), low),
+            pltpu.VMEM((rows, width), low),
+            pltpu.VMEM((chips, part, rows), low),
+            pltpu.VMEM((chips, part, rows), low),
+            pltpu.VMEM((rows, width), low),
+            pltpu.VMEM((2, own_rows, 8 * rows), low),
+            pltpu.VMEM((8, rows), jnp.float32),
+            pltpu.VMEM((8, rows), jnp.float32),
+            pltpu.VMEM((groups, 1, width), jnp.float32),
+            pltpu.VMEM((chips, own_rows, part), low),
+            pltpu.VMEM((chips, own_rows, part), low),
+            dma((4,)),
+            dma((chips,)),
+            dma((2, chips)),
+            dma((2, chips)),
+            dma((2, 1)),
+            dma((2, 8, 2)),
+            dma((2, 2, 8)),
+            dma((2, groups)),
+            dma((2, chips)),
+            dma((2, 8)),
+            dma((2, 5)),
+            dma((2, 3)),
+            dma((chips,)),
+        ],
+        compiler_params=pltpu.CompilerParams(
+            collective_id=0, has_side_effects=True, vmem_limit_bytes=66 * 1000 * 1000
+        ),
+        name="trunk",
+    )(att, res, ups, rg, gain, weight, probs, q, k, v)
+
+
 def sum_groups(groups, value):
     if groups & (groups - 1):
         return lax.psum(value, "dp")
@@ -150,6 +638,21 @@
 
     observed = jnp.sum((action_mask == 0).astype(jnp.int32), axis=1)
     probs, attended = attend(observed, query_rows, key_rows, value_rows)
+    if pair and groups == 16 and attended.shape[0] == LEN:
+        out = trunk(
+            groups,
+            attended,
+            residual,
+            upstream,
+            residual_grad,
+            norm_gain[None, :],
+            out_weight,
+            probs[0],
+            query_rows,
+            key_rows,
+            value_rows,
+        )
+        return (*out[:6], out[6][0])
     attended_all = lax.all_gather(attended, "dp", axis=0, tiled=True)
     if pair:
         theirs = dot(attended, weight_rows(1 - mine), NT).astype(jnp.bfloat16)

time: 297 us -> 228 us (0.77); the launches traced: 293 us -> 227 us
  Pallas kernels: 26.9 us -> 208 us
  waiting for transfers between devices: 145 us -> 0 us
  matrix products: 72.5 us -> 0 us
  starting transfers between devices: 15.3 us -> 0 us
  between operations: 14.2 us -> 0.65 us
  other arithmetic: 8.16 us -> 2.65 us
  local copies, waits for them, and re-layouts: 11 us -> 15.5 us
    pallas_call x1, Pallas kernels: 13.9 us -> 195 us  [trunk(): pl.pallas_call(functools.partial(trunk_kernel, groups), in_specs=[anywher...]
    ppermute x7 -> x0, waiting for transfers between devices: 145 us -> none  [the longest x4 59.5 us: sum_groups(): lax.ppermute(value, 'dp', [(i, i ^ bit) for i in range(groups)])]
    dot_general x5 -> x0, matrix products: 72.5 us -> none  [the longest x3 52.4 us: dot(): return lax.dot_general(a, b, dims, preferred_element_type=jnp.float32)]
    unnamed x12 -> x16, local copies, waits for them, and re-layouts: 0.03 us -> 14.2 us
    all_to_all x1 -> x0, starting transfers between devices: 8.79 us -> none  [shards(): lax.all_to_all(grad_full, 'dp', split_axis=1, concat_axis=0, tiled=True)]
    ppermute x7 -> x0, starting transfers between devices: 6.5 us -> none  [the longest x4 2.64 us: sum_groups(): lax.ppermute(value, 'dp', [(i, i ^ bit) for i in range(groups)])]
    concatenate x1 -> x0, local copies, waits for them, and re-layouts: 6.28 us -> none  [shards(): grad_full = jnp.concatenate([low_half, high_half], axis=1)]
    all_to_all x1 -> x0, local copies, waits for them, and re-layouts: 4.68 us -> none  [shards(): lax.all_to_all(grad_full, 'dp', split_axis=1, concat_axis=0, tiled=True)]
  transfers between devices with their start and end apart: 9 -> 0, of which waited for: 7 -> 0; matrix products, arithmetic and copies ran while one was open for 25% -> 0% of each run, Pallas kernels for 5% -> 0%
where the time goes in v1:
time: 228 us; the launch traced here: 227 us
  Pallas kernels  208 us (91%)
  local copies, waits for them, and re-layouts  15.5 us (7%)
  other arithmetic  2.65 us (1%)
    pallas_call x1, Pallas kernels, trunk(): pl.pallas_call(functools.partial(trunk_kernel, groups), in_specs=[anywher...  195 us
    unnamed x16, local copies, waits for them, and re-layouts  14.2 us
    pallas_call x1, Pallas kernels, attend(): pl.pallas_call(functools.partial(forward_kernel, heads), grid=(seq_count,...  13 us

profile of v1, /device:TPU:27, one launch (start us, length us, event | category | flops | bytes accessed | tf_op | source)
XLA Modules:
  0.0 227.1 jit_solution(10439425957861926639)
XLA Ops:
  0.6 1.3 fusion
  2.0 1.3 broadcast_in_dim.3.gain_ref
  3.3 13.0 %attend.1 = (bf16[1,20,384,384]{3,2,1,0:T(8,128)(2,1)}, bf16[384,2560]{1,0:T(8,128)(2,1)}) custom-call(s32[1]{0:T(128)} %bitcast.observed_ref, bf16[384,2560]{1,0:T(8,128)(2,1)} %q_h.1, bf16[384,2560]{1,0:T(8,128)(2,1)} %k_h.1, bf16[384,2560]{1,0:T(8,128)(2,1)} %v_h.1), custom_call_target="tpu_custom_call" | custom-call | flops 1509949440 | bytes 13762560 | tf_op jit(solution)/shard_map/attend/pallas_call | solution.py:75
  16.3 195.3 %trunk.1 = (bf16[384,2560]{1,0:T(8,128)(2,1)}, bf16[384,2560]{1,0:T(8,128)(2,1)}, bf16[384,2560]{1,0:T(8,128)(2,1)}, bf16[384,2560]{1,0:T(8,128)(2,1)}, bf16[384...) custom-call(bf16[384,2560]{1,0:T(8,128)(2,1)} %get-tuple-element.16.att_h, ...), custom_call_target="tpu_custom_call" | custom-call | tf_op jit(solution)/shard_map/trunk/pallas_call | solution.py:554
  211.6 1.3 reduce.1
  212.9 0.0 copy-start.4
  212.9 3.1 %copy.22 = bf16[384,2560]{1,0:T(8,128)(2,1)} copy(bf16[384,2560]{1,0:T(8,128)(2,1)} %get-tuple-element.32) | data formatting | bytes 3932160
  216.0 0.0 copy-done.4
  216.0 0.0 copy-start.3
  216.0 1.3 copy.23
  217.3 1.0 copy-done.3
  218.3 0.0 copy-start.2
  218.3 1.3 copy.24
  219.6 1.0 copy-done.2
  220.5 0.0 copy-start.1
  220.5 1.3 copy.25
  221.8 1.0 copy-done.1
  222.8 0.0 copy-start
  222.8 1.3 copy.26
  224.1 1.4 copy-done
  225.4 1.7 copy.27
Async XLA Ops:
  212.9 3.1 %copy-start.4 = (bf16[384,2560]{1,0:T(8,128)(2,1)S(1)}, bf16[384,2560]{1,0:T(8,128)(2,1)}, u32[]{:S(2)}) copy-start(bf16[384,2560]{1,0:T(8,128)(2,1)} %get-tuple-element.33) | copy-start | bytes 5898244
  216.0 2.3 copy-start.3
  218.3 2.3 copy-start.2
  220.5 2.3 copy-start.1
  222.8 2.6 %copy-start = (f32[320,2560]{1,0:T(8,128)S(1)}, f32[320,2560]{1,0:T(8,128)}, u32[]{:S(2)}) copy-start(f32[320,2560]{1,0:T(8,128)} %get-tuple-element.37) | copy-start | bytes 9830404

commit v2 on v1

--- a/solution.py
+++ b/solution.py
@@ -116,13 +116,12 @@
 
 def trunk_kernel(
     groups,
-    att_h,
+    mask_ref,
+    gain_h,
     res_h,
     ups_h,
     rg_h,
-    gain_ref,
     w_h,
-    probs_h,
     q_h,
     k_h,
     v_h,
@@ -131,12 +130,15 @@
     gq_h,
     gk_h,
     gv_h,
-    gw_h,
+    kept_h,
+    mid_in,
     gain_o,
     gath,
     att_v,
+    probs_v,
     ups_v,
     rg_v,
+    gain_ref,
     theirs,
     arrived,
     lo_v,
@@ -144,12 +146,13 @@
     turned,
     turned_other,
     other_v,
+    wp,
+    cotangent_sum,
     pieces,
     sums_mine,
     sums_theirs,
     gain_v,
     mid_out,
-    mid_in,
     load_sem,
     w_sem,
     p_sems,
@@ -226,38 +229,92 @@
             def _():
                 pltpu.make_async_copy(src, pieces.at[kind, :, 0:rows], piece_sems.at[1, kind, 0]).start()
 
-    def projection(wp, res_v):
-        def w_load(side, k):
-            start = pl.multiple_of(side * width + k * part, part)
-            return pltpu.make_async_copy(w_h.at[pl.ds(start, part), :], wp.at[k], w_sem.at[k])
-
-        att_load = pltpu.make_async_copy(att_h, att_v, load_sem.at[0])
-        att_load.start()
-        for k in range(chips):
-            w_load(1 - t, k).start()
+    gain_ref[...] = jnp.reshape(gain_h[...], (1, width))
+    two = 2 * HEAD_DIM
+    steps = width // two
+
+    def head_cols(i):
+        return pl.ds(pl.multiple_of(i * two, 128), two)
+
+    def attend_loop(qb, kb, vb):
+        observed = jnp.sum((mask_ref[...] == 0).astype(jnp.int32), axis=1, keepdims=True)
+        row = lax.broadcasted_iota(jnp.int32, (rows, rows), 0)
+        column = lax.broadcasted_iota(jnp.int32, (rows, rows), 1)
+        allowed = column <= jnp.maximum(row, observed - 1)
+
+        def fetch(i, slot):
+            return [
+                pltpu.make_async_copy(a.at[:, head_cols(i)], b.at[slot], fetch_sem.at[slot, j])
+                for j, (a, b) in enumerate(((q_h, qb), (k_h, kb), (v_h, vb)))
+            ]
+
+        def step(i, carry):
+            slot = i % 2
+
+            @pl.when(i + 1 < steps)
+            def _():
+                for copy in fetch(i + 1, 1 - slot):
+                    copy.start()
+
+            for copy in fetch(i, slot):
+                copy.wait()
+
+            @pl.when(i >= steps - chips)
+            def _():
+                w_load(1 - t, i - (steps - chips)).start()
+
+            parts = []
+            for j in range(2):
+                span = slice(j * HEAD_DIM, (j + 1) * HEAD_DIM)
+                scores = dot(qb[slot, :, span], kb[slot, :, span], NT) * SCALE
+                masked = jnp.where(allowed, scores, -jnp.inf)
+                weights = jnp.exp(masked - jnp.max(masked, axis=1, keepdims=True))
+                probs = weights * (1.0 / jnp.sum(weights, axis=1, keepdims=True))
+                low = probs.astype(jnp.bfloat16)
+                probs_v[2 * i + j] = low
+                parts.append(jnp.dot(low, vb[slot, :, span], preferred_element_type=jnp.float32))
+            att_v[:, head_cols(i)] = jnp.concatenate(parts, axis=1).astype(jnp.bfloat16)
+            return carry
+
+        return fetch, step
+
+    def send_half(side):
+        gather(att_v, 4, side, z_peer).start()
+        gather(att_v, 2, side, x_peer).start()
+        gather(att_v, 1, side, core_peer).start()
+
+    def w_load(side, k):
+        start = pl.multiple_of(side * width + k * part, part)
+        return pltpu.make_async_copy(w_h.at[pl.ds(start, part), :], w_rows(k), w_sem.at[k])
+
+    def w_rows(k):
+        return wp.at[pl.ds(pl.multiple_of(k * part, part), part), :]
+
+    def projection(res_v, qb, kb, vb):
+        fetch, step = attend_loop(qb, kb, vb)
+        for copy in fetch(0, 0):
+            copy.start()
         later = [
             pltpu.make_async_copy(a, b, load_sem.at[i + 1])
             for i, (a, b) in enumerate(((res_h, res_v), (ups_h, ups_v), (rg_h, rg_v)))
         ]
-        for copy in later:
-            copy.start()
+        lax.fori_loop(0, steps // 2 + 1, step, 0)
         pl.semaphore_wait(barrier, groups)
-        gather(att_h, 4, 0, z_peer).start()
-        gather(att_h, 2, 1, x_peer).start()
-        gather(att_h, 4, 1, z_peer).start()
-        gather(att_h, 2, 0, x_peer).start()
-        for side in (0, 1):
-            gather(att_h, 1, side, core_peer).start()
-        att_load.wait()
+        send_half(0)
+        lax.fori_loop(steps // 2 + 1, steps, step, 0)
 
         def give(k, carry):
             w_load(1 - t, k).wait()
-            theirs[k] = dot(att_v[...], wp[k], NT).astype(jnp.bfloat16)
+            theirs[k] = dot(att_v[...], w_rows(k)[...], NT).astype(jnp.bfloat16)
             remote(theirs.at[k], arrived.at[k], p_sems, (k,), y_peer).start()
             w_load(t, k).start()
             return carry
 
-        lax.fori_loop(0, chips, give, 0)
+        lax.fori_loop(0, 1, give, 0)
+        send_half(1)
+        for copy in later:
+            copy.start()
+        lax.fori_loop(1, chips, give, 0)
         for copy in later:
             copy.wait()
 
@@ -265,7 +322,7 @@
             squares, inner = carry
             cols = pl.ds(pl.multiple_of(k * part, 128), part)
             w_load(t, k).wait()
-            own = dot(att_v[...], wp[k], NT)
+            own = dot(att_v[...], w_rows(k)[...], NT)
             remote(theirs.at[k], arrived.at[k], p_sems, (k,), y_peer).wait()
             total = own + arrived[k].astype(jnp.float32)
             low = (total + res_v[:, cols].astype(jnp.float32)).astype(jnp.bfloat16)
@@ -278,19 +335,22 @@
 
         zero = jnp.zeros((rows, 1), jnp.float32)
         carry = lax.fori_loop(0, 2, take, (zero, zero))
-        gather(att_h, 4, 0, z_peer).wait_recv()
+        gather(att_v, 4, 0, z_peer).wait_recv()
         gather(gath.at[4], 6, 0, x_peer).start()
-        gather(att_h, 2, 1, x_peer).wait_recv()
+        carry = lax.fori_loop(2, 3, take, carry)
+        gather(att_v, 2, 1, x_peer).wait_recv()
         gather(gath.at[2], 6, 1, z_peer).start()
-        squares, inner = lax.fori_loop(2, chips, take, carry)
+        squares, inner = lax.fori_loop(3, chips, take, carry)
         lane = lax.broadcasted_iota(jnp.int32, (rows, 128), 1)
         packed = jnp.where(lane == 0, squares, jnp.where(lane == 1, inner, 0.0))
         sums_mine[...] = jnp.transpose(packed)[0:8]
 
     pl.run_scoped(
         projection,
-        pltpu.VMEM((chips, part, width), jnp.bfloat16),
         pltpu.VMEM((rows, width), jnp.bfloat16),
+        pltpu.VMEM((2, rows, two), jnp.bfloat16),
+        pltpu.VMEM((2, rows, two), jnp.bfloat16),
+        pltpu.VMEM((2, rows, two), jnp.bfloat16),
     )
     exchange = remote(sums_mine, sums_theirs, s_sems, (0,), y_peer)
     exchange.start()
@@ -305,7 +365,10 @@
     row_inner = inner / (rms * model)
     slope = row_inner * inverse
 
-    def normalise(k, carry):
+    native_kept = 1 - (zh + t) % 2
+
+    def normalise(step_index, carry):
+        k = (step_index // 2 * (1 - 2 * t) + t) * 2 + step_index % 2
         cols = pl.ds(pl.multiple_of(k * part, 128), part)
         out = lo_v[:, cols].astype(jnp.float32)
         ups = ups_v[:, cols].astype(jnp.float32)
@@ -315,8 +378,12 @@
         turned[k] = jnp.transpose(grad.astype(jnp.float32)).astype(jnp.bfloat16)
         gain_v[d, :, cols] = jnp.sum(ups * (out * inverse), axis=0, keepdims=True)
         remote(turned.at[k], turned_other.at[k], g_sems, (k,), y_peer).start()
-        for dc in (0, 1):
-            piece(0, turned, k, dc)
+
+        @pl.when(native_kept == 0)
+        def _():
+            for dc in (0, 1):
+                piece(0, turned, k, dc)
+
         return carry
 
     lax.fori_loop(0, chips, normalise, 0)
@@ -328,40 +395,60 @@
 
     for r in range(1, groups):
         gain_copy(r, d).start()
+    gather(att_v, 4, 1, z_peer).wait_recv()
+    gather(att_v, 2, 0, x_peer).wait_recv()
     for side in (0, 1):
-        if side == 1:
-            gather(att_h, 4, 1, z_peer).wait_recv()
         gather(gath.at[4], 5, side, core_peer).start()
-        if side == 0:
-            gather(att_h, 2, 0, x_peer).wait_recv()
         gather(gath.at[2], 3, side, core_peer).start()
 
-    def pass_on(k, carry):
-        remote(turned.at[k], turned_other.at[k], g_sems, (k,), y_peer).wait()
+    def cotangent_own(k, carry):
+        cols = pl.ds(pl.multiple_of(k * part, 128), part)
+        cotangent_sum[:, cols] = jnp.dot(
+            gr_v[...], wp[:, cols], preferred_element_type=jnp.float32
+        )
+        return carry
+
+    lax.fori_loop(0, chips, cotangent_own, 0)
+    for k in range(chips):
+        w_load(1 - t, k).start()
+
+    def pass_on(step_index, carry):
+        k = (1 - t + step_index // 2 * (2 * t - 1)) * 2 + step_index % 2
+        remote(turned.at[k], turned_other.at[k], g_sems, (k,), y_peer).wait_recv()
         for dc in (0, 1):
             piece(1, turned_other, k, dc)
-        cols = pl.ds(pl.multiple_of(k * part, 128), part)
-        other_v[:, cols] = jnp.transpose(turned_other[k].astype(jnp.float32)).astype(jnp.bfloat16)
+
+        other_v[...] = jnp.transpose(turned_other[k].astype(jnp.float32)).astype(jnp.bfloat16)
+        w_load(1 - t, k).wait()
+
+        def add_columns(cb, carry):
+            cols = pl.ds(pl.multiple_of(cb * part, 128), part)
+            cotangent_sum[:, cols] += jnp.dot(
+                other_v[...], w_rows(k)[:, cols], preferred_element_type=jnp.float32
+            )
+            return carry
+
+        lax.fori_loop(0, chips, add_columns, 0)
         return carry
 
-    lax.fori_loop(0, 2, pass_on, 0)
+    lax.fori_loop(0, 1, pass_on, 0)
     for side in (0, 1):
         gather(gath.at[4], 6, side, x_peer).wait_recv()
         gather(gath.at[6], 7, side, core_peer).start()
-    lax.fori_loop(2, chips, pass_on, 0)
+    lax.fori_loop(1, 2, pass_on, 0)
     for slot in (1, 3, 5, 7):
         for side in (0, 1):
-            gather(att_h, slot, side, core_peer).wait_recv()
+            gather(att_v, slot, side, core_peer).wait_recv()
 
     blocks = width // part
-    keeps_first = (zh + t) % 2 == 0
+    far_chip = (zp + 1 - t) % 2
 
     def finish(kept, att_b):
         def block_load(cb, slot):
             cols = pl.ds(pl.multiple_of(cb * part, 128), part)
             copies = [
                 pltpu.make_async_copy(
-                    att_h.at[:, cols], att_b.at[slot, 0:rows, :], block_sem.at[slot, 0]
+                    att_v.at[:, cols], att_b.at[slot, 0:rows, :], block_sem.at[slot, 0]
                 )
             ]
             for delta in range(1, 8):
@@ -377,28 +464,28 @@
         def mid_copy(cb):
             return remote(mid_out.at[cb], mid_in.at[cb], mid_sems, (cb,), mid_peer)
 
-        for copy in block_load(0, 0):
-            copy.start()
-        for kind in (0, 1):
+        def kept_copy(cb):
+            cols = pl.ds(pl.multiple_of(cb * part, 128), part)
+            return pltpu.make_async_copy(kept.at[cb], kept_h.at[:, cols], final_sem.at[cb])
+
+        def multiply(kind):
+            for copy in block_load(0, 0):
+                copy.start()
             for delta in range(8):
                 pltpu.make_async_copy(
                     turned.at[0, 0:own_rows, :],
                     pieces.at[kind, :, delta * rows : (delta + 1) * rows],
                     piece_sems.at[1, kind, delta],
                 ).wait()
-            keeps = keeps_first if kind == 0 else jnp.logical_not(keeps_first)
-
-            def product(cb, carry, kind=kind, keeps=keeps):
+            keeps = (kind + native_kept) % 2 == 1
+
+            def product(cb, carry):
                 slot = cb % 2
-                if kind == 0:
-                    for copy in block_load((cb + 1) % blocks, 1 - slot):
+
+                @pl.when(cb + 1 < blocks)
+                def _():
+                    for copy in block_load(cb + 1, 1 - slot):
                         copy.start()
-                else:
-
-                    @pl.when(cb + 1 < blocks)
-                    def _():
-                        for copy in block_load(cb + 1, 1 - slot):
-                            copy.start()
 
                 for copy in block_load(cb, slot):
                     copy.wait()
@@ -407,6 +494,7 @@
                 @pl.when(keeps)
                 def _():
                     kept[cb] = value
+                    kept_copy(cb).start()
 
                 @pl.when(jnp.logical_not(keeps))
                 def _():
@@ -417,17 +505,25 @@
 
             lax.fori_loop(0, blocks, product, 0)
 
-        def attention(pb, qb, kb, vb, wc, ob):
-            steps = width // (2 * HEAD_DIM)
-
+        @pl.when(native_kept == 0)
+        def _():
+            multiply(0)
+
+        lax.fori_loop(2, chips, pass_on, 0)
+
+        @pl.when(native_kept == 1)
+        def _():
+            for k in range(chips):
+                for dc in (0, 1):
+                    piece(0, turned, k, dc)
+
+        def attention(qb, kb, vb, ob):
             def fetch(i, slot):
                 cols = pl.ds(pl.multiple_of(i * 2 * HEAD_DIM, 128), 2 * HEAD_DIM)
                 pairs = (
-                    (probs_h.at[pl.ds(2 * i, 2)], pb),
                     (q_h.at[:, cols], qb),
                     (k_h.at[:, cols], kb),
                     (v_h.at[:, cols], vb),
-                    (w_h.at[:, cols], wc),
                 )
                 return [
                     pltpu.make_async_copy(a, b.at[slot], fetch_sem.at[slot, j])
@@ -460,15 +556,10 @@
                     for copy in emit(i - 2, slot):
                         copy.wait()
 
-                mine = wc[slot, pl.ds(pl.multiple_of(t * width, 128), width), :]
-                other = wc[slot, pl.ds(pl.multiple_of((1 - t) * width, 128), width), :]
-                cotangents = (
-                    jnp.dot(gr_v[...], mine, preferred_element_type=jnp.float32)
-                    + jnp.dot(other_v[...], other, preferred_element_type=jnp.float32)
-                ).astype(jnp.bfloat16)
+                cotangents = cotangent_sum[:, head_cols(i)].astype(jnp.bfloat16)
                 for j in range(2):
                     span = slice(j * HEAD_DIM, (j + 1) * HEAD_DIM)
-                    low = pb[slot, j]
+                    low = probs_v[2 * i + j]
                     cotangent = cotangents[:, span]
                     ob[slot, 2, :, span] = dot(low, cotangent, TN).astype(jnp.bfloat16)
                     grad_probs = dot(cotangent, vb[slot, :, span], NT)
@@ -485,19 +576,24 @@
                     copy.start()
                 return carry
 
-            lax.fori_loop(0, steps, step, 0)
+            early = 2 * far_chip
+            lax.fori_loop(0, early, step, 0)
+
+            @pl.when(native_kept == 1)
+            def _():
+                multiply(1)
+
+            lax.fori_loop(early, steps, step, 0)
+            multiply(1 - native_kept)
             for i in (steps - 2, steps - 1):
                 for copy in emit(i, i % 2):
                     copy.wait()
 
-        two = 2 * HEAD_DIM
         pl.run_scoped(
             attention,
-            pltpu.VMEM((2, 2, rows, rows), jnp.bfloat16),
             pltpu.VMEM((2, rows, two), jnp.bfloat16),
             pltpu.VMEM((2, rows, two), jnp.bfloat16),
             pltpu.VMEM((2, rows, two), jnp.bfloat16),
-            pltpu.VMEM((2, model, two), jnp.bfloat16),
             pltpu.VMEM((2, 3, rows, two), jnp.bfloat16),
         )
         for r in range(1, groups):
@@ -505,19 +601,11 @@
         total = gain_v[0]
         for i in range(1, groups):
             total = total + gain_v[i]
-        gain_o[...] = total
-
-        def close(cb, carry):
+        gain_o[...] = jnp.reshape(total, (width,))
+
+        for cb in range(blocks):
             mid_copy(cb).wait()
-            kept[cb] = kept[cb] + mid_in[cb].astype(jnp.float32)
-            cols = pl.ds(pl.multiple_of(cb * part, 128), part)
-            pltpu.make_async_copy(kept.at[cb], gw_h.at[:, cols], final_sem.at[cb]).start()
-            return carry
-
-        lax.fori_loop(0, blocks, close, 0)
-        for cb in range(blocks):
-            cols = slice(cb * part, (cb + 1) * part)
-            pltpu.make_async_copy(kept.at[cb], gw_h.at[:, cols], final_sem.at[cb]).wait()
+            kept_copy(cb).wait()
 
     pl.run_scoped(
         finish,
@@ -526,9 +614,11 @@
     )
     lo_out.wait()
     gr_out.wait()
+    for k in range(chips):
+        remote(turned.at[k], turned_other.at[k], g_sems, (k,), y_peer).wait_send()
     for slot in range(1, 8):
         for side in (0, 1):
-            gather(att_h, slot, side, core_peer).wait_send()
+            gather(att_v, slot, side, core_peer).wait_send()
     for kind in (0, 1):
         for delta in range(1, 8):
             remote(
@@ -540,12 +630,13 @@
             ).wait_send()
 
 
-def trunk(groups, att, res, ups, rg, gain, weight, probs, q, k, v):
-    rows, width = att.shape
+def trunk(groups, mask, gain, res, ups, rg, weight, q, k, v):
+    rows, width = q.shape
     model = weight.shape[0]
     chips = 4
     part = width // chips
     own_rows = part // 2
+    two = 2 * HEAD_DIM
     anywhere = pl.BlockSpec(memory_space=pl.ANY)
     local = pl.BlockSpec(memory_space=pltpu.VMEM)
     low = jnp.bfloat16
@@ -553,30 +644,34 @@
     dma = pltpu.SemaphoreType.DMA
     return pl.pallas_call(
         functools.partial(trunk_kernel, groups),
-        in_specs=[anywhere] * 4 + [local] + [anywhere] * 5,
-        out_specs=[anywhere] * 6 + [local, anywhere],
+        in_specs=[local] * 2 + [anywhere] * 7,
+        out_specs=[anywhere] * 7 + [local, anywhere],
         out_shape=[act] * 5
         + [
             jax.ShapeDtypeStruct((own_rows, width), jnp.float32),
-            jax.ShapeDtypeStruct((1, width), jnp.float32),
+            jax.ShapeDtypeStruct((chips, own_rows, part), low),
+            jax.ShapeDtypeStruct((width,), jnp.float32),
             jax.ShapeDtypeStruct((8, rows, width), low),
         ],
         scratch_shapes=[
             pltpu.VMEM((rows, width), low),
+            pltpu.VMEM((width // HEAD_DIM, rows, rows), low),
             pltpu.VMEM((rows, width), low),
             pltpu.VMEM((rows, width), low),
+            pltpu.VMEM((1, width), jnp.float32),
             pltpu.VMEM((chips, rows, part), low),
             pltpu.VMEM((chips, rows, part), low),
             pltpu.VMEM((rows, width), low),
             pltpu.VMEM((rows, width), low),
             pltpu.VMEM((chips, part, rows), low),
             pltpu.VMEM((chips, part, rows), low),
-            pltpu.VMEM((rows, width), low),
+            pltpu.VMEM((rows, part), low),
+            pltpu.VMEM((width, width), low),
+            pltpu.VMEM((rows, width), jnp.float32),
             pltpu.VMEM((2, own_rows, 8 * rows), low),
             pltpu.VMEM((8, rows), jnp.float32),
             pltpu.VMEM((8, rows), jnp.float32),
             pltpu.VMEM((groups, 1, width), jnp.float32),
-            pltpu.VMEM((chips, own_rows, part), low),
             pltpu.VMEM((chips, own_rows, part), low),
             dma((4,)),
             dma((chips,)),
@@ -588,7 +683,7 @@
             dma((2, groups)),
             dma((2, chips)),
             dma((2, 8)),
-            dma((2, 5)),
+            dma((2, 4)),
             dma((2, 3)),
             dma((chips,)),
         ],
@@ -596,7 +691,30 @@
             collective_id=0, has_side_effects=True, vmem_limit_bytes=66 * 1000 * 1000
         ),
         name="trunk",
-    )(att, res, ups, rg, gain, weight, probs, q, k, v)
+    )(mask, gain, res, ups, rg, weight, q, k, v)
+
+
+def hand_out_kernel(*refs):
+    for a, b in zip(refs[:5], refs[7:12]):
+        b[...] = a[...]
+    refs[12][...] = refs[5][...] + refs[6][...].astype(jnp.float32)
+
+
+def hand_out(arrays, kept, arrived):
+    rows, width = arrays[0].shape
+    own_rows = kept.shape[0]
+    steps, part = arrived.shape[0], arrived.shape[2]
+    act = pl.BlockSpec((rows // steps, width), lambda i: (i, 0))
+    column = pl.BlockSpec((own_rows, part), lambda i: (0, i))
+    return pl.pallas_call(
+        hand_out_kernel,
+        grid=(steps,),
+        in_specs=[act] * 5 + [column, pl.BlockSpec((None, own_rows, part), lambda i: (i, 0, 0))],
+        out_specs=[act] * 5 + [column],
+        out_shape=[jax.ShapeDtypeStruct((rows, width), jnp.bfloat16)] * 5
+        + [jax.ShapeDtypeStruct((own_rows, width), jnp.float32)],
+        name="hand_out",
+    )(*arrays, kept, arrived)
 
 
 def sum_groups(groups, value):
@@ -636,23 +754,22 @@
             return value + lax.ppermute(value, "tensor", swap)
         return lax.psum(value, "tensor")
 
-    observed = jnp.sum((action_mask == 0).astype(jnp.int32), axis=1)
-    probs, attended = attend(observed, query_rows, key_rows, value_rows)
-    if pair and groups == 16 and attended.shape[0] == LEN:
+    if pair and groups == 16 and query_rows.shape[0] == LEN:
         out = trunk(
             groups,
-            attended,
+            action_mask,
+            norm_gain,
             residual,
             upstream,
             residual_grad,
-            norm_gain[None, :],
             out_weight,
-            probs[0],
             query_rows,
             key_rows,
             value_rows,
         )
-        return (*out[:6], out[6][0])
+        return (*hand_out(out[:5], out[5], out[6]), out[7])
+    observed = jnp.sum((action_mask == 0).astype(jnp.int32), axis=1)
+    probs, attended = attend(observed, query_rows, key_rows, value_rows)
     attended_all = lax.all_gather(attended, "dp", axis=0, tiled=True)
     if pair:
         theirs = dot(attended, weight_rows(1 - mine), NT).astype(jnp.bfloat16)

time: 228 us -> 200 us (0.88); the launches traced: 227 us -> 196 us
  local copies, waits for them, and re-layouts: 15.5 us -> 0.61 us
  Pallas kernels: 208 us -> 195 us
  other arithmetic: 2.65 us -> 0 us
    unnamed x16 -> x3, local copies, waits for them, and re-layouts: 14.2 us -> 0.61 us
    pallas_call x2, Pallas kernels: 208 us -> 195 us  [the longest x1 185 us: trunk(): pl.pallas_call(functools.partial(trunk_kernel, groups), in_specs=[local]...]
where the time goes in v2:
time: 200 us; the launch traced here: 196 us
  Pallas kernels  195 us (98%)
    pallas_call x1, Pallas kernels, trunk(): pl.pallas_call(functools.partial(trunk_kernel, groups), in_specs=[local]...  185 us
    pallas_call x1, Pallas kernels, hand_out(): pl.pallas_call(hand_out_kernel, grid=(steps,), in_specs=[act] * 5 + [colu...  9.7 us

profile of v2, /device:TPU:27, one launch (start us, length us, event | category | flops | bytes accessed | tf_op | source)
XLA Modules:
  0.0 196.1 jit_solution(262037791479487483)
XLA Ops:
  0.6 185.1 %trunk.1 = (bf16[384,2560]{1,0:T(8,128)(2,1)}, bf16[384,2560]{1,0:T(8,128)(2,1)}, bf16[384,2560]{1,0:T(8,128)(2,1)}, bf16[384,2560]{1,0:T(8,128)(2,1)}, bf16[384...) custom-call(s32[1,384]{1,0:T(1,128)} %mask_ref.1, ...), custom_call_target="tpu_custom_call" | custom-call | tf_op jit(solution)/shard_map/trunk/pallas_call | solution.py:645
  185.7 0.0 copy-start
  185.8 9.7 %hand_out.1 = (bf16[384,2560]{1,0:T(8,128)(2,1)}, bf16[384,2560]{1,0:T(8,128)(2,1)}, bf16[384,2560]{1,0:T(8,128)(2,1)}, bf16[384,2560]{1,0:T(8,128)(2,1)}, bf16[...) custom-call(bf16[384,2560]{1,0:T(8,128)(2,1)} %get-tuple-element.21.refs_0_, bf16[384,2560]{1,0:T(8,128)(2,1)} %get-tuple-element.22.refs_1_, ...), custom_call_target="tpu_custom_call" | custom-call | tf_op jit(solution)/shard_map/hand_out/pallas_call | solution.py:709
  195.5 0.0 copy-done
  195.5 0.6 copy.17
Async XLA Ops:
  185.7 9.7 %copy-start = (f32[2560]{0:T(1024)S(1)}, f32[2560]{0:T(1024)}, u32[]{:S(2)}) copy-start(f32[2560]{0:T(1024)} %get-tuple-element.48) | copy-start | bytes 30724

commit v3 on v2

--- a/solution.py
+++ b/solution.py
@@ -379,7 +379,7 @@
         gain_v[d, :, cols] = jnp.sum(ups * (out * inverse), axis=0, keepdims=True)
         remote(turned.at[k], turned_other.at[k], g_sems, (k,), y_peer).start()
 
-        @pl.when(native_kept == 0)
+        @pl.when(native_kept * (step_index // 2) == 0)
         def _():
             for dc in (0, 1):
                 piece(0, turned, k, dc)
@@ -412,11 +412,18 @@
     for k in range(chips):
         w_load(1 - t, k).start()
 
+    def arrival(step_index):
+        return (1 - t + step_index // 2 * (2 * t - 1)) * 2 + step_index % 2
+
     def pass_on(step_index, carry):
-        k = (1 - t + step_index // 2 * (2 * t - 1)) * 2 + step_index % 2
+        k = arrival(step_index)
         remote(turned.at[k], turned_other.at[k], g_sems, (k,), y_peer).wait_recv()
-        for dc in (0, 1):
-            piece(1, turned_other, k, dc)
+
+        @pl.when(native_kept + step_index // 2 > 0)
+        def _():
+            for dc in (0, 1):
+                piece(1, turned_other, k, dc)
+
 
         other_v[...] = jnp.transpose(turned_other[k].astype(jnp.float32)).astype(jnp.bfloat16)
         w_load(1 - t, k).wait()
@@ -508,14 +515,23 @@
         @pl.when(native_kept == 0)
         def _():
             multiply(0)
-
-        lax.fori_loop(2, chips, pass_on, 0)
+            for i in (0, 1):
+                for dc in (0, 1):
+                    piece(1, turned_other, arrival(i), dc)
+
+        lax.fori_loop(2, 3, pass_on, 0)
+
+        @pl.when(native_kept * (1 - far_chip) == 1)
+        def _():
+            multiply(1)
+
+        lax.fori_loop(3, chips, pass_on, 0)
 
         @pl.when(native_kept == 1)
         def _():
-            for k in range(chips):
+            for i in (0, 1):
                 for dc in (0, 1):
-                    piece(0, turned, k, dc)
+                    piece(0, turned, arrival(i), dc)
 
         def attention(qb, kb, vb, ob):
             def fetch(i, slot):
@@ -579,7 +595,7 @@
             early = 2 * far_chip
             lax.fori_loop(0, early, step, 0)
 
-            @pl.when(native_kept == 1)
+            @pl.when(native_kept * far_chip == 1)
             def _():
                 multiply(1)
 

time: 200 us -> 195 us (0.975); the launches traced: 196 us -> 194 us
  Pallas kernels: 195 us -> 193 us
    pallas_call x1, Pallas kernels: 185 us -> 183 us  [trunk(): pl.pallas_call(functools.partial(trunk_kernel, groups), in_specs=[local]...]
where the time goes in v3:
time: 195 us; the launch traced here: 194 us
  Pallas kernels  193 us (99%)
    pallas_call x1, Pallas kernels, trunk(): pl.pallas_call(functools.partial(trunk_kernel, groups), in_specs=[local]...  183 us
    pallas_call x1, Pallas kernels, hand_out(): pl.pallas_call(hand_out_kernel, grid=(steps,), in_specs=[act] * 5 + [colu...  9.7 us

profile of v3, /device:TPU:27, one launch (start us, length us, event | category | flops | bytes accessed | tf_op | source)
XLA Modules:
  0.0 194.0 jit_solution(11015418677280485665)
XLA Ops:
  0.6 183.0 %trunk.1 = (bf16[384,2560]{1,0:T(8,128)(2,1)}, bf16[384,2560]{1,0:T(8,128)(2,1)}, bf16[384,2560]{1,0:T(8,128)(2,1)}, bf16[384,2560]{1,0:T(8,128)(2,1)}, bf16[384...) custom-call(s32[1,384]{1,0:T(1,128)} %mask_ref.1, ...), custom_call_target="tpu_custom_call" | custom-call | tf_op jit(solution)/shard_map/trunk/pallas_call | solution.py:661
  183.6 0.0 copy-start
  183.6 9.7 %hand_out.1 = (bf16[384,2560]{1,0:T(8,128)(2,1)}, bf16[384,2560]{1,0:T(8,128)(2,1)}, bf16[384,2560]{1,0:T(8,128)(2,1)}, bf16[384,2560]{1,0:T(8,128)(2,1)}, bf16[...) custom-call(bf16[384,2560]{1,0:T(8,128)(2,1)} %get-tuple-element.21.refs_0_, bf16[384,2560]{1,0:T(8,128)(2,1)} %get-tuple-element.22.refs_1_, ...), custom_call_target="tpu_custom_call" | custom-call | tf_op jit(solution)/shard_map/hand_out/pallas_call | solution.py:725
  193.4 0.0 copy-done
  193.4 0.6 copy.17
Async XLA Ops:
  183.6 9.7 %copy-start = (f32[2560]{0:T(1024)S(1)}, f32[2560]{0:T(1024)}, u32[]{:S(2)}) copy-start(f32[2560]{0:T(1024)} %get-tuple-element.48) | copy-start | bytes 30724
